TPU v7x, 32 devices: a whole 2x2x4 slice. The times are simulated.
32 devices in a mesh: cell: 8 (over z, x), grp: 4 (over y, core).
Axes of the slice: x: 2, y: 2, z: 4, core: 2. Of those that a mesh axis runs over, the one named last changes fastest.
Arguments:
- atom_sites: float32 [3, 16384], P(None, ('cell', 'grp')), may hold values from 0 to 8, as said below
- grid_points: float32 [3, 12288], P(None, ('cell', 'grp')), may hold values from 0 to 8, as said below
- dipole_guess: float32 [3, 16384], P(None, ('cell', 'grp')), may hold values from -2 to 2
- fixed_field: float32 [3, 16384], P(None, ('cell', 'grp')), may hold values from -1800 to 1800
- polarisability: float32 [16384], P(('cell', 'grp')), may hold values from 0.0005 to 0.002
- base_charge: float32 [12288], P(('cell', 'grp')), may hold values from -12 to 12
- response: float32 [12288], P(('cell', 'grp')), may hold values from 0.02 to 0.2
- near_blocks: int32 [128, 8], P(('cell', 'grp')), may hold values from 0 to 47, as said below
- grid_blocks: int32 [128, 4], P(('cell', 'grp')), may hold values from 0 to 35, as said below
- source_blocks: int32 [96, 8], P(('cell', 'grp')), may hold values from 0 to 47, as said below
Outputs:
- dipoles: float32 [3, 16384], P(None, ('cell', 'grp'))
- qm_charges: float32 [12288], P(('cell', 'grp'))
Inputs may be any that keep to these rules, and one draw needn't show every extreme that they name: `atom_sites`: atom a has first coordinate in [c, c + 1) with c = a // 2048, the other two in [0, 1). `grid_points`: grid point g has first coordinate in [c, c + 1) with c = g // 1536, the other two in [0, 1). `near_blocks`: each row holds 8 distinct MM window indices, never the block's own index 16 + b % 16. `grid_blocks`: each row holds 4 distinct grid window indices. `source_blocks`: each row holds 8 distinct MM window indices.
All inputs are finite; a program needn't handle non-finite values.
Results may differ from a plain program's by a relative error of at most 0.0003.
Values sent between devices are 32-bit elements; how exact they have to be, the bound alone decides.
A program may use at most 64 MiB of HBM per device.

v0:
```python
import jax
import jax.numpy as jnp
from jax import lax
from jax.sharding import PartitionSpec as P

BLOCK = 128
ITERS = 3
soften_sq = 0.04


def with_halo(x, sides, width):
    for axis, dim in sides:
        peers, length = (lax.axis_size(axis), x.shape[dim])
        up = [(i, (i + 1) % peers) for i in range(peers - 1)]
        down = [(j, i) for i, j in up]
        last = lax.slice_in_dim(x, length - width, length, axis=dim)
        initial = lax.slice_in_dim(x, 0, width, axis=dim)
        before = lax.ppermute(last, axis, up)
        after = lax.ppermute(initial, axis, down)
        x = jnp.concatenate([before, x, after], axis=dim)
    return x


def pair_geometry(targets, sources):
    delta_x = targets[0][:, None] - sources[0][None, :]
    delta_y = targets[1][:, None] - sources[1][None, :]
    delta_z = targets[2][:, None] - sources[2][None, :]
    inverse = 1.0 / jnp.sqrt(delta_x * delta_x + delta_y * delta_y + delta_z * delta_z + soften_sq)
    inv_cube = inverse * inverse * inverse
    return (delta_x, delta_y, delta_z, inv_cube, inv_cube * inverse * inverse)


def dipole_field(targets, sources, moments, keep_mask):
    delta_x, delta_y, delta_z, inv_cube, inv_fifth = pair_geometry(targets, sources)
    projected = (
        moments[0][None, :] * delta_x
        + moments[1][None, :] * delta_y
        + moments[2][None, :] * delta_z
    )
    radial = 3.0 * projected * inv_fifth * keep_mask
    direct = inv_cube * keep_mask
    return jnp.stack(
        [
            jnp.sum(radial * delta_x - moments[0][None, :] * direct, axis=1),
            jnp.sum(radial * delta_y - moments[1][None, :] * direct, axis=1),
            jnp.sum(radial * delta_z - moments[2][None, :] * direct, axis=1),
        ]
    )


def charge_field(targets, sources, charges):
    delta_x, delta_y, delta_z, inv_cube, inv_fifth = pair_geometry(targets, sources)
    weight = charges[None, :] * inv_cube
    return jnp.stack(
        [
            jnp.sum(weight * delta_x, axis=1),
            jnp.sum(weight * delta_y, axis=1),
            jnp.sum(weight * delta_z, axis=1),
        ]
    )


def dipole_potential(targets, sources, moments):
    delta_x, delta_y, delta_z, inv_cube, inv_fifth = pair_geometry(targets, sources)
    projected = (
        moments[0][None, :] * delta_x
        + moments[1][None, :] * delta_y
        + moments[2][None, :] * delta_z
    )
    return jnp.sum(projected * inv_cube, axis=1)


def far_geometry(targets, cell_here, cell_count):
    centres = jnp.arange(cell_count, dtype=jnp.int32).astype(jnp.float32) + 0.5
    delta_x = targets[0][None, :] - centres[:, None]
    delta_y = targets[1][None, :] - 0.5
    delta_z = targets[2][None, :] - 0.5
    far_mask = (jnp.abs(jnp.arange(cell_count, dtype=jnp.int32) - cell_here) >= 2).astype(
        jnp.float32
    )[:, None]
    inverse = 1.0 / jnp.sqrt(delta_x * delta_x + delta_y * delta_y + delta_z * delta_z + soften_sq)
    inv_cube = inverse * inverse * inverse * far_mask
    return (delta_x, delta_y, delta_z, inv_cube, inv_cube * inverse * inverse)


def far_field(targets, cell_here, moments, charges):
    delta_x, delta_y, delta_z, inv_cube, inv_fifth = far_geometry(
        targets, cell_here, charges.shape[0]
    )
    projected = moments[:, 0:1] * delta_x + moments[:, 1:2] * delta_y + moments[:, 2:3] * delta_z
    radial = 3.0 * projected * inv_fifth
    coulomb = charges[:, None] * inv_cube
    return jnp.stack(
        [
            jnp.sum(radial * delta_x - moments[:, 0:1] * inv_cube + coulomb * delta_x, axis=0),
            jnp.sum(radial * delta_y - moments[:, 1:2] * inv_cube + coulomb * delta_y, axis=0),
            jnp.sum(radial * delta_z - moments[:, 2:3] * inv_cube + coulomb * delta_z, axis=0),
        ]
    )


def far_potential(targets, cell_here, moments):
    delta_x, delta_y, delta_z, inv_cube, inv_fifth = far_geometry(
        targets, cell_here, moments.shape[0]
    )
    projected = moments[:, 0:1] * delta_x + moments[:, 1:2] * delta_y + moments[:, 2:3] * delta_z
    return jnp.sum(projected * inv_cube, axis=0)


def listed_tiles(tile_set, index_lists):
    taken = jnp.take(tile_set, index_lists, axis=1)
    count, listed = index_lists.shape
    return jnp.transpose(taken, (1, 0, 2, 3)).reshape(count, 3, listed * tile_set.shape[2])


def spread(payload):
    lifted = payload[:, None, None, :]
    with_rims = with_halo(lifted, (("cell", 1),), 1)
    return lax.all_gather(with_rims, "grp", axis=2, tiled=True)


def body(
    atom_sites,
    grid_points,
    dipole_guess,
    fixed_field,
    polarisability,
    base_charge,
    response,
    near_blocks,
    grid_blocks,
    source_blocks,
):
    groups = lax.axis_size("grp")
    cell_here = lax.axis_index("cell")
    grp_here = lax.axis_index("grp")
    local_blocks = near_blocks.shape[0]
    local_gblocks = source_blocks.shape[0]
    atom_count = atom_sites.shape[1]
    grid_count = grid_points.shape[1]
    cell_blocks = local_blocks * groups
    cell_gblocks = local_gblocks * groups
    statics = spread(jnp.concatenate([atom_sites, grid_points], axis=1))
    site_tiles = statics[:, :, :, :atom_count].reshape(3, 3 * cell_blocks, BLOCK)
    point_tiles = statics[:, :, :, atom_count:].reshape(3, 3 * cell_gblocks, BLOCK)
    atom_targets = jnp.transpose(atom_sites.reshape(3, local_blocks, BLOCK), (1, 0, 2))
    grid_targets = jnp.transpose(grid_points.reshape(3, local_gblocks, BLOCK), (1, 0, 2))
    own_slots = cell_blocks + grp_here * local_blocks + jnp.arange(local_blocks, dtype=jnp.int32)
    atom_lists = jnp.concatenate([own_slots[:, None], near_blocks], axis=1)
    near_sites = listed_tiles(site_tiles, atom_lists)
    grid_sites = listed_tiles(point_tiles, grid_blocks)
    source_sites = listed_tiles(site_tiles, source_blocks)
    keep_mask = jnp.concatenate(
        [
            1.0 - jnp.eye(BLOCK, dtype=jnp.float32),
            jnp.ones((BLOCK, near_blocks.shape[1] * BLOCK), jnp.float32),
        ],
        axis=1,
    )
    centre = jnp.stack(
        [
            cell_here.astype(jnp.float32) + 0.5,
            jnp.array(0.5, jnp.float32),
            jnp.array(0.5, jnp.float32),
        ]
    )
    offsets = grid_points - centre[:, None]
    dipoles = dipole_guess
    charges = base_charge
    for iteration in range(ITERS):
        shared = spread(jnp.concatenate([dipoles, charges.reshape(3, grid_count // 3)], axis=1))
        dipole_tiles = shared[:, :, :, :atom_count].reshape(3, 3 * cell_blocks, BLOCK)
        charge_tiles = jnp.transpose(shared[:, :, :, atom_count:], (1, 2, 0, 3)).reshape(
            3 * cell_gblocks, BLOCK
        )
        local_sums = jnp.concatenate(
            [
                jnp.sum(dipoles, axis=1),
                jnp.sum(charges)[None],
                jnp.sum(charges[None, :] * offsets, axis=1),
            ]
        )
        cell_sums = lax.psum(local_sums, "grp")
        moment_table = lax.all_gather(cell_sums[None, :], "cell", axis=0, tiled=True)
        dipole_sums = moment_table[:, 0:3]
        charge_sums = moment_table[:, 3]
        moments = dipole_sums + moment_table[:, 4:7]
        near_dipoles = listed_tiles(dipole_tiles, atom_lists)
        source_dipoles = listed_tiles(dipole_tiles, source_blocks)
        grid_charges = jnp.take(charge_tiles, grid_blocks, axis=0).reshape(local_blocks, -1)

        def one_atom_block(block_args):
            targets, sources, source_moments, points, point_charges = block_args
            accumulated = dipole_field(targets, sources, source_moments, keep_mask)
            accumulated = accumulated + charge_field(targets, points, point_charges)
            return accumulated + far_field(targets, cell_here, moments, charge_sums)

        def one_grid_block(block_args):
            targets, sources, source_moments = block_args
            return dipole_potential(targets, sources, source_moments) + far_potential(
                targets, cell_here, dipole_sums
            )

        induced_field = lax.map(
            one_atom_block, (atom_targets, near_sites, near_dipoles, grid_sites, grid_charges)
        )
        induced_field = jnp.transpose(induced_field, (1, 0, 2)).reshape(3, atom_count)
        potential = lax.map(one_grid_block, (grid_targets, source_sites, source_dipoles)).reshape(
            grid_count
        )
        dipoles = polarisability[None, :] * (fixed_field + induced_field)
        charges = base_charge - response * potential
    return (dipoles, charges)


def solution(mesh):
    return jax.shard_map(
        body,
        mesh=mesh,
        in_specs=(
            P(None, ("cell", "grp")),
            P(None, ("cell", "grp")),
            P(None, ("cell", "grp")),
            P(None, ("cell", "grp")),
            P(("cell", "grp")),
            P(("cell", "grp")),
            P(("cell", "grp")),
            P(("cell", "grp"), None),
            P(("cell", "grp"), None),
            P(("cell", "grp"), None),
        ),
        out_specs=(P(None, ("cell", "grp")), P(("cell", "grp"))),
        check_vma=False,
    )
```

profile of v0, /device:TPU:0, one launch (start us, length us, event | category | flops | bytes accessed | tf_op | source)
XLA Modules:
  0.0 166.5 jit_solution(10735519480641597523)
XLA Ops:
  0.6 0.7 maximum_bitcast_fusion.1
  1.4 1.3 collective-permute-start.1
  2.7 5.5 %collective-permute-start = (f32[3,1,1,640]{3,0,2,1:T(4,128)S(1)}, f32[3,1,1,640]{3,0,2,1:T(4,128)S(1)}, u32[]{:S(2)}, u32[]{:S(2)}) collective-permute-start(f32[3,1,1,640]{3,0,2,1:T(4,128)S(1)} %maximum_bitcast_fusion.1), channel_id=1, source_target_pairs={{0,4},{4,8},{8,12},{12,16},{16,20},{20,24},{24,28},{1,5},{5,9},{9,... | collective-permute-start | bytes 23048 | tf_op jit(solution)/shard_map/ppermute | solution.py:18
  8.2 1.3 collective-permute-start.3
  9.5 5.4 %collective-permute-start.2 = (f32[3,1,1,896]{3,0,2,1:T(4,128)S(1)}, f32[3,1,1,896]{3,0,2,1:T(4,128)S(1)}, u32[]{:S(2)}, u32[]{:S(2)}) collective-permute-start(f32[3,1,1,896]{3,0,2,1:T(4,128)S(1)} %maximum_bitcast_fusion), channel_id=1, source_target_pairs={{0,4},{4,8},{8,12},{12,16},{16,20},{20,24},{24,28},{1,5},{5,9},{9,... | collective-permute-start | bytes 32264 | tf_op jit(solution)/shard_map/ppermute | solution.py:18
  15.0 0.7 copy-done.8
  15.8 0.7 copy-done.2
  17.3 0.7 maximum_bitcast_fusion.4
  18.0 5.7 %psum.21 = f32[1,7]{1,0:T(1,128)S(1)} all-reduce(f32[1,7]{1,0:T(1,128)S(1)} %maximum_bitcast_fusion.4), channel_id=1, replica_groups=mesh['cell'=8,'grp'=4] {'grp'}, use_global_device_ids=true, to_apply=%region_3.6 | all-reduce | flops 7 | bytes 56 | tf_op jit(solution)/shard_map/psum | solution.py:183
  23.8 0.7 copy-done.9
  24.8 19.3 %all-gather = f32[8,1,7]{2,1,0:T(1,128)S(1)} all-gather(f32[1,1,7]{2,1,0:T(1,128)S(1)} %bitcast.636), channel_id=1, replica_groups=mesh['cell'=8,'grp'=4] {'cell'}, dimensions={0}, use_global_device_ids=true | all-gather | bytes 252 | tf_op jit(solution)/shard_map/all_gather | solution.py:184
  44.6 5.4 %all_gather.21 = f32[3,3,4,640]{3,0,2,1:T(4,128)S(1)} all-gather(f32[3,3,1,640]{3,0,2,1:T(4,128)S(1)} %pad_maximum_fusion.1), channel_id=1, replica_groups=mesh['cell'=8,'grp'=4] {'grp'}, dimensions={2}, use_global_device_ids=true | all-gather | bytes 115200 | tf_op jit(solution)/shard_map/all_gather | solution.py:119
  51.3 0.6 gather_fusion.1
  51.9 5.6 %all_gather.22 = f32[3,3,4,896]{3,0,2,1:T(4,128)S(1)} all-gather(f32[3,3,1,896]{3,0,2,1:T(4,128)S(1)} %pad_maximum_fusion), channel_id=1, replica_groups=mesh['cell'=8,'grp'=4] {'grp'}, dimensions={2}, use_global_device_ids=true | all-gather | bytes 161280 | tf_op jit(solution)/shard_map/all_gather | solution.py:119
  58.1 0.6 gather_fusion.2
  59.7 2.4 %while.79 = (s32[]{:T(128)}, f32[3,128]{1,0:T(4,128)S(1)}, f32[3,3,1024]{2,0,1:T(4,128)S(1)}, f32[3,3,128]{2,1,0:T(4,128)S(1)}, f32[3,3,1024]{2,1,0:T(4,128)S(1)...) while((s32[]{:T(128)}, f32[3,128]{1,0:T(4,128)S(1)}, ...), condition=%wide.region_18.22_spmd, body=%wide.region_15.21_spmd.sunk | while | flops 2375092 | bytes 91217 | solution.py:208
  62.1 0.6 fusion.190
  63.1 6.3 %while.78 = (s32[]{:T(128)}, f32[4,3,128]{2,1,0:T(4,128)S(1)}, f32[4,3,1152]{2,1,0:T(4,128)S(1)}, f32[4,3,128]{2,1,0:T(4,128)S(1)}, f32[4,3,1152]{2,1,0:T(4,128)...) while((s32[]{:T(128)}, f32[4,3,128]{2,1,0:T(4,128)S(1)}, ...), condition=%wide.region_14.17_spmd, body=%wide.region_4.16_spmd.sunk | while | flops 6232500 | bytes 724117 | solution.py:204
  63.7 0.9 fusion.208
  65.3 0.9 fusion.208
  66.9 0.9 fusion.208
  68.5 0.9 fusion.208
  69.6 1.3 collective-permute-start.5
  70.9 0.7 maximum_bitcast_fusion.5
  71.5 4.5 %collective-permute-start.4 = (f32[3,1,1,640]{3,0,2,1:T(4,128)S(1)}, f32[3,1,1,640]{3,0,2,1:T(4,128)S(1)}, u32[]{:S(2)}, u32[]{:S(2)}) collective-permute-start(f32[3,1,1,640]{3,0,2,1:T(4,128)S(1)} %maximum_bitcast_fusion.2), channel_id=1, source_target_pairs={{0,4},{4,8},{8,12},{12,16},{16,20},{20,24},{24,28},{1,5},{5,9},{9,... | collective-permute-start | bytes 23048 | tf_op jit(solution)/shard_map/ppermute | solution.py:18
  76.1 7.0 %psum.22 = f32[1,7]{1,0:T(1,128)S(1)} all-reduce(f32[1,7]{1,0:T(1,128)S(1)} %maximum_bitcast_fusion.5), channel_id=1, replica_groups=mesh['cell'=8,'grp'=4] {'grp'}, use_global_device_ids=true, to_apply=%region_22.26 | all-reduce | flops 7 | bytes 56 | tf_op jit(solution)/shard_map/psum | solution.py:183
  83.1 16.3 %all-gather.1 = f32[8,1,7]{2,1,0:T(1,128)S(1)} all-gather(f32[1,1,7]{2,1,0:T(1,128)S(1)} %bitcast.637), channel_id=1, replica_groups=mesh['cell'=8,'grp'=4] {'cell'}, dimensions={0}, use_global_device_ids=true | all-gather | bytes 252 | tf_op jit(solution)/shard_map/all_gather | solution.py:184
  99.8 5.4 %all_gather.24 = f32[3,3,4,640]{3,0,2,1:T(4,128)S(1)} all-gather(f32[3,3,1,640]{3,0,2,1:T(4,128)S(1)} %pad_maximum_fusion.2), channel_id=1, replica_groups=mesh['cell'=8,'grp'=4] {'grp'}, dimensions={2}, use_global_device_ids=true | all-gather | bytes 115200 | tf_op jit(solution)/shard_map/all_gather | solution.py:119
  105.9 0.6 gather_fusion.6
  107.3 6.3 %while.80 = (s32[]{:T(128)}, f32[4,3,128]{2,1,0:T(4,128)S(1)}, f32[4,3,1152]{2,1,0:T(4,128)S(1)}, f32[4,3,128]{2,1,0:T(4,128)S(1)}, f32[4,3,1152]{2,1,0:T(4,128)...) while((s32[]{:T(128)}, f32[4,3,128]{2,1,0:T(4,128)S(1)}, ...), condition=%wide.region_33.37_spmd, body=%wide.region_23.36_spmd.sunk | while | flops 6232500 | bytes 724117 | solution.py:204
  108.0 0.9 fusion.213
  109.6 0.9 fusion.213
  111.2 0.9 fusion.213
  112.8 0.9 fusion.213
  113.8 2.4 %while.81 = (s32[]{:T(128)}, f32[3,128]{1,0:T(4,128)S(1)}, f32[3,3,1024]{2,0,1:T(4,128)S(1)}, f32[3,3,128]{2,1,0:T(4,128)S(1)}, f32[3,3,1024]{2,1,0:T(4,128)S(1)...) while((s32[]{:T(128)}, f32[3,128]{1,0:T(4,128)S(1)}, ...), condition=%wide.region_37.41_spmd, body=%wide.region_34.40_spmd.sunk | while | flops 2375092 | bytes 91217 | solution.py:208
  117.1 1.3 collective-permute-start.7
  118.4 0.7 maximum_bitcast_fusion.6
  119.1 4.5 %collective-permute-start.6 = (f32[3,1,1,640]{3,0,2,1:T(4,128)S(1)}, f32[3,1,1,640]{3,0,2,1:T(4,128)S(1)}, u32[]{:S(2)}, u32[]{:S(2)}) collective-permute-start(f32[3,1,1,640]{3,0,2,1:T(4,128)S(1)} %maximum_bitcast_fusion.3), channel_id=1, source_target_pairs={{0,4},{4,8},{8,12},{12,16},{16,20},{20,24},{24,28},{1,5},{5,9},{9,... | collective-permute-start | bytes 23048 | tf_op jit(solution)/shard_map/ppermute | solution.py:18
  123.6 5.8 %psum.23 = f32[1,7]{1,0:T(1,128)S(1)} all-reduce(f32[1,7]{1,0:T(1,128)S(1)} %maximum_bitcast_fusion.6), channel_id=1, replica_groups=mesh['cell'=8,'grp'=4] {'grp'}, use_global_device_ids=true, to_apply=%region_41.45 | all-reduce | flops 7 | bytes 56 | tf_op jit(solution)/shard_map/psum | solution.py:183
  129.4 19.2 %all-gather.2 = f32[8,1,7]{2,1,0:T(1,128)S(1)} all-gather(f32[1,1,7]{2,1,0:T(1,128)S(1)} %bitcast.638), channel_id=1, replica_groups=mesh['cell'=8,'grp'=4] {'cell'}, dimensions={0}, use_global_device_ids=true | all-gather | bytes 252 | tf_op jit(solution)/shard_map/all_gather | solution.py:184
  149.0 5.4 %all_gather.26 = f32[3,3,4,640]{3,0,2,1:T(4,128)S(1)} all-gather(f32[3,3,1,640]{3,0,2,1:T(4,128)S(1)} %pad_maximum_fusion.3), channel_id=1, replica_groups=mesh['cell'=8,'grp'=4] {'grp'}, dimensions={2}, use_global_device_ids=true | all-gather | bytes 115200 | tf_op jit(solution)/shard_map/all_gather | solution.py:119
  155.0 0.6 gather_fusion.9
  156.5 6.3 %while.82 = (s32[]{:T(128)}, f32[4,3,128]{2,1,0:T(4,128)S(1)}, f32[4,3,1152]{2,1,0:T(4,128)S(1)}, f32[4,3,128]{2,1,0:T(4,128)S(1)}, f32[4,3,1152]{2,1,0:T(4,128)...) while((s32[]{:T(128)}, f32[4,3,128]{2,1,0:T(4,128)S(1)}, ...), condition=%wide.region_52.56_spmd, body=%wide.region_42.55_spmd.sunk | while | flops 6232500 | bytes 724117 | solution.py:204
  157.2 0.9 fusion.218
  158.7 0.9 fusion.218
  160.3 0.9 fusion.218
  161.9 0.9 fusion.218
  163.5 2.4 %while.83 = (s32[]{:T(128)}, f32[3,128]{1,0:T(4,128)S(1)}, f32[3,3,1024]{2,0,1:T(4,128)S(1)}, f32[3,3,128]{2,1,0:T(4,128)S(1)}, f32[3,3,1024]{2,1,0:T(4,128)S(1)...) while((s32[]{:T(128)}, f32[3,128]{1,0:T(4,128)S(1)}, ...), condition=%wide.region_56.60_spmd, body=%wide.region_53.59_spmd.sunk | while | flops 2375092 | bytes 91217 | solution.py:208
  (370 shorter events, 24.8 us)
Async XLA Ops:
  0.6 7.5 %copy-start = (f32[3,384]{1,0:T(4,128)S(1)}, f32[3,384]{1,0:T(4,128)}, u32[]{:S(2)}) copy-start(f32[3,384]{1,0:T(4,128)} %param.29) | copy-start | bytes 13828
  0.6 7.5 %copy-start.1 = (f32[3,512]{1,0:T(4,128)S(1)}, f32[3,512]{1,0:T(4,128)}, u32[]{:S(2)}) copy-start(f32[3,512]{1,0:T(4,128)} %param.28) | copy-start | bytes 18436
  1.4 43.2 %collective-permute-start.1 = (f32[3,1,1,640]{3,0,2,1:T(4,128)S(1)}, f32[3,1,1,640]{3,0,2,1:T(4,128)S(1)}, u32[]{:S(2)}, u32[]{:S(2)}) collective-permute-start(f32[3,1,1,640]{3,0,2,1:T(4,128)S(1)} %maximum_bitcast_fusion.1), channel_id=1, source_target_pairs={{4,0},{8,4},{12,8},{16,12},{20,16},{24,20},{28,24},{5,1},{9,5},{13... | collective-permute-start | bytes 23048 | tf_op jit(solution)/shard_map/ppermute | solution.py:19
  2.7 41.9 %collective-permute-start = (f32[3,1,1,640]{3,0,2,1:T(4,128)S(1)}, f32[3,1,1,640]{3,0,2,1:T(4,128)S(1)}, u32[]{:S(2)}, u32[]{:S(2)}) collective-permute-start(f32[3,1,1,640]{3,0,2,1:T(4,128)S(1)} %maximum_bitcast_fusion.1), channel_id=1, source_target_pairs={{0,4},{4,8},{8,12},{12,16},{16,20},{20,24},{24,28},{1,5},{5,9},{9,... | collective-permute-start | bytes 23048 | tf_op jit(solution)/shard_map/ppermute | solution.py:18
  8.2 6.8 %copy-start.7 = (s32[4,4]{1,0:T(4,128)S(1)}, s32[4,4]{1,0:T(4,128)}, u32[]{:S(2)}) copy-start(s32[4,4]{1,0:T(4,128)} %param.36) | copy-start | bytes 196
  8.2 43.7 %collective-permute-start.3 = (f32[3,1,1,896]{3,0,2,1:T(4,128)S(1)}, f32[3,1,1,896]{3,0,2,1:T(4,128)S(1)}, u32[]{:S(2)}, u32[]{:S(2)}) collective-permute-start(f32[3,1,1,896]{3,0,2,1:T(4,128)S(1)} %maximum_bitcast_fusion), channel_id=1, source_target_pairs={{4,0},{8,4},{12,8},{16,12},{20,16},{24,20},{28,24},{5,1},{9,5},{13... | collective-permute-start | bytes 32264 | tf_op jit(solution)/shard_map/ppermute | solution.py:19
  9.5 42.4 %collective-permute-start.2 = (f32[3,1,1,896]{3,0,2,1:T(4,128)S(1)}, f32[3,1,1,896]{3,0,2,1:T(4,128)S(1)}, u32[]{:S(2)}, u32[]{:S(2)}) collective-permute-start(f32[3,1,1,896]{3,0,2,1:T(4,128)S(1)} %maximum_bitcast_fusion), channel_id=1, source_target_pairs={{0,4},{4,8},{8,12},{12,16},{16,20},{20,24},{24,28},{1,5},{5,9},{9,... | collective-permute-start | bytes 32264 | tf_op jit(solution)/shard_map/ppermute | solution.py:18
  15.0 0.7 copy-start.8
  15.7 0.7 copy-start.2
  15.7 1.3 copy-start.4
  23.8 0.7 copy-start.9
  59.6 2.4 %copy-start.5 = (f32[384]{0:T(512)S(1)}, f32[384]{0:T(512)}, u32[]{:S(2)}) copy-start(f32[384]{0:T(512)} %param.34) | copy-start | bytes 4612
  63.0 6.4 %copy-start.3 = (f32[3,512]{1,0:T(4,128)S(1)}, f32[3,512]{1,0:T(4,128)}, u32[]{:S(2)}) copy-start(f32[3,512]{1,0:T(4,128)} %param.31) | copy-start | bytes 18436
  63.0 6.4 %copy-start.6 = (f32[512]{0:T(512)S(1)}, f32[512]{0:T(512)}, u32[]{:S(2)}) copy-start(f32[512]{0:T(512)} %param.32) | copy-start | bytes 6148
  69.6 30.3 %collective-permute-start.5 = (f32[3,1,1,640]{3,0,2,1:T(4,128)S(1)}, f32[3,1,1,640]{3,0,2,1:T(4,128)S(1)}, u32[]{:S(2)}, u32[]{:S(2)}) collective-permute-start(f32[3,1,1,640]{3,0,2,1:T(4,128)S(1)} %maximum_bitcast_fusion.2), channel_id=1, source_target_pairs={{4,0},{8,4},{12,8},{16,12},{20,16},{24,20},{28,24},{5,1},{9,5},{13... | collective-permute-start | bytes 23048 | tf_op jit(solution)/shard_map/ppermute | solution.py:19
  71.5 28.3 %collective-permute-start.4 = (f32[3,1,1,640]{3,0,2,1:T(4,128)S(1)}, f32[3,1,1,640]{3,0,2,1:T(4,128)S(1)}, u32[]{:S(2)}, u32[]{:S(2)}) collective-permute-start(f32[3,1,1,640]{3,0,2,1:T(4,128)S(1)} %maximum_bitcast_fusion.2), channel_id=1, source_target_pairs={{0,4},{4,8},{8,12},{12,16},{16,20},{20,24},{24,28},{1,5},{5,9},{9,... | collective-permute-start | bytes 23048 | tf_op jit(solution)/shard_map/ppermute | solution.py:18
  117.1 31.9 %collective-permute-start.7 = (f32[3,1,1,640]{3,0,2,1:T(4,128)S(1)}, f32[3,1,1,640]{3,0,2,1:T(4,128)S(1)}, u32[]{:S(2)}, u32[]{:S(2)}) collective-permute-start(f32[3,1,1,640]{3,0,2,1:T(4,128)S(1)} %maximum_bitcast_fusion.3), channel_id=1, source_target_pairs={{4,0},{8,4},{12,8},{16,12},{20,16},{24,20},{28,24},{5,1},{9,5},{13... | collective-permute-start | bytes 23048 | tf_op jit(solution)/shard_map/ppermute | solution.py:19
  119.1 29.9 %collective-permute-start.6 = (f32[3,1,1,640]{3,0,2,1:T(4,128)S(1)}, f32[3,1,1,640]{3,0,2,1:T(4,128)S(1)}, u32[]{:S(2)}, u32[]{:S(2)}) collective-permute-start(f32[3,1,1,640]{3,0,2,1:T(4,128)S(1)} %maximum_bitcast_fusion.3), channel_id=1, source_target_pairs={{0,4},{4,8},{8,12},{12,16},{16,20},{20,24},{24,28},{1,5},{5,9},{9,... | collective-permute-start | bytes 23048 | tf_op jit(solution)/shard_map/ppermute | solution.py:18
where the time goes:
time: 167 us; the launch traced here: 166 us
  blocking collectives  95.1 us (57%)
  other arithmetic  30.4 us (18%)
  starting transfers between devices  25.2 us (15%)
  local copies, waits for them, and re-layouts  13.1 us (8%)
    all_gather x3, blocking collectives, body(): lax.all_gather(cell_sums[None, :], 'cell', axis=0, tiled=True)  54.8 us
    all_gather x4, blocking collectives, spread(): return lax.all_gather(with_rims, 'grp', axis=2, tiled=True)  21.7 us
    ppermute x4, starting transfers between devices, with_halo(): before = lax.ppermute(last, axis, up)  20 us
    psum x3, blocking collectives, body(): cell_sums = lax.psum(local_sums, 'grp')  18.6 us
    reduce_sum x12, other arithmetic, dipole_field(): jnp.sum(radial * delta_x - moments[0][None, :] * direct, axis=1)  10.7 us
    gather x10, local copies, waits for them, and re-layouts, listed_tiles(): taken = jnp.take(tile_set, index_lists, axis=1)  5.42 us
    ppermute x4, starting transfers between devices, with_halo(): after = lax.ppermute(initial, axis, down)  5.16 us
    reduce_sum x9, other arithmetic, dipole_potential(): return jnp.sum(projected * inv_cube, axis=1)  4.71 us
  transfers between devices with their start and end apart: 8, of which 0 were waited for; matrix products, arithmetic and copies ran while one was open for 4% of the time, Pallas kernels for 0%

commit v1 on v0

--- a/solution.py
+++ b/solution.py
@@ -180,7 +180,7 @@
                 jnp.sum(charges[None, :] * offsets, axis=1),
             ]
         )
-        cell_sums = lax.psum(local_sums, "grp")
+        cell_sums = jnp.sum(lax.all_gather(local_sums, "grp"), axis=0)
         moment_table = lax.all_gather(cell_sums[None, :], "cell", axis=0, tiled=True)
         dipole_sums = moment_table[:, 0:3]
         charge_sums = moment_table[:, 3]

time: 167 us -> 174 us (1.042)
  local copies, waits for them, and re-layouts: 13.1 us -> 16.1 us
  blocking collectives: 95.1 us -> 97.5 us
    unnamed x0 -> x6, blocking collectives: none -> 75.8 us
    all_gather x3 -> x0, blocking collectives: 54.8 us -> none  [body(): lax.all_gather(cell_sums[None, :], 'cell', axis=0, tiled=True)]
    psum x3 -> x0, blocking collectives: 18.6 us -> none  [body(): cell_sums = lax.psum(local_sums, 'grp')]
    unnamed x23 -> x38, local copies, waits for them, and re-layouts: 2.06 us -> 4.57 us
    unnamed x3 -> x6, other arithmetic: 0.23 us -> 2.64 us
    broadcast_in_dim x3 -> x0, other arithmetic: 2.13 us -> none  [body(): cell_sums[None, :]]
  transfers between devices with their start and end apart: 8 -> 8, of which waited for: 0 -> 0; matrix products, arithmetic and copies ran while one was open for 4% -> 5% of each run, Pallas kernels for 0% -> 0%
where the time goes in v1:
time: 174 us
  blocking collectives  97.5 us (56%)
  other arithmetic  30.7 us (18%)
  starting transfers between devices  25.2 us (14%)
  local copies, waits for them, and re-layouts  16.1 us (9%)
  between operations  2.54 us (1%)
    unnamed x6, blocking collectives  75.8 us
    all_gather x4, blocking collectives, spread(): return lax.all_gather(with_rims, 'grp', axis=2, tiled=True)  21.7 us
    ppermute x4, starting transfers between devices, with_halo(): before = lax.ppermute(last, axis, up)  20 us
    reduce_sum x12, other arithmetic, dipole_field(): jnp.sum(radial * delta_x - moments[0][None, :] * direct, axis=1)  10.7 us
    gather x10, local copies, waits for them, and re-layouts, listed_tiles(): taken = jnp.take(tile_set, index_lists, axis=1)  5.42 us
    ppermute x4, starting transfers between devices, with_halo(): after = lax.ppermute(initial, axis, down)  5.16 us
    reduce_sum x9, other arithmetic, dipole_potential(): return jnp.sum(projected * inv_cube, axis=1)  4.71 us
    unnamed x38, local copies, waits for them, and re-layouts  4.57 us
  transfers between devices with their start and end apart: 8, of which 0 were waited for; matrix products, arithmetic and copies ran while one was open for 5% of the time, Pallas kernels for 0%

profile of v1, /device:TPU:0, one launch (start us, length us, event | category | flops | bytes accessed | tf_op | source)
XLA Modules:
  0.0 173.7 jit_solution(18302989412209890871)
XLA Ops:
  0.6 0.7 maximum_bitcast_fusion.1
  1.4 1.3 collective-permute-start.1
  2.7 5.5 %collective-permute-start = (f32[3,1,1,640]{3,0,2,1:T(4,128)S(1)}, f32[3,1,1,640]{3,0,2,1:T(4,128)S(1)}, u32[]{:S(2)}, u32[]{:S(2)}) collective-permute-start(f32[3,1,1,640]{3,0,2,1:T(4,128)S(1)} %maximum_bitcast_fusion.1), channel_id=1, source_target_pairs={{0,4},{4,8},{8,12},{12,16},{16,20},{20,24},{24,28},{1,5},{5,9},{9,... | collective-permute-start | bytes 23048 | tf_op jit(solution)/shard_map/ppermute | solution.py:18
  8.2 1.3 collective-permute-start.3
  9.5 5.4 %collective-permute-start.2 = (f32[3,1,1,896]{3,0,2,1:T(4,128)S(1)}, f32[3,1,1,896]{3,0,2,1:T(4,128)S(1)}, u32[]{:S(2)}, u32[]{:S(2)}) collective-permute-start(f32[3,1,1,896]{3,0,2,1:T(4,128)S(1)} %maximum_bitcast_fusion), channel_id=1, source_target_pairs={{0,4},{4,8},{8,12},{12,16},{16,20},{20,24},{24,28},{1,5},{5,9},{9,... | collective-permute-start | bytes 32264 | tf_op jit(solution)/shard_map/ppermute | solution.py:18
  15.0 0.7 copy-done.8
  15.8 0.7 copy-done.2
  17.7 0.7 dynamic-slice.1
  20.5 0.8 maximum_dynamic-update-slice_fusion
  21.3 5.7 %all-reduce.2 = f32[28]{0:T(128)S(1)} all-reduce(f32[28]{0:T(128)S(1)} %maximum_dynamic-update-slice_fusion), channel_id=2, replica_groups=mesh['cell'=8,'grp'=4] {'grp'}, use_global_device_ids=true, to_apply=%add.2 | all-reduce | flops 28 | bytes 224
  27.4 20.1 %all-reduce.3 = f32[56]{0:T(128)S(1)} all-reduce(f32[56]{0:T(128)S(1)} %dynamic-update-slice.1), channel_id=3, replica_groups=mesh['cell'=8,'grp'=4] {'cell'}, use_global_device_ids=true, to_apply=%add.3 | all-reduce | flops 56 | bytes 448
  47.5 0.7 copy-done.9
  49.1 5.4 %all_gather.39 = f32[3,3,4,640]{3,0,2,1:T(4,128)S(1)} all-gather(f32[3,3,1,640]{3,0,2,1:T(4,128)S(1)} %pad_maximum_fusion.1), channel_id=1, replica_groups=mesh['cell'=8,'grp'=4] {'grp'}, dimensions={2}, use_global_device_ids=true | all-gather | bytes 115200 | tf_op jit(solution)/shard_map/all_gather | solution.py:119
  55.8 0.6 gather_fusion.1
  56.5 5.6 %all_gather.40 = f32[3,3,4,896]{3,0,2,1:T(4,128)S(1)} all-gather(f32[3,3,1,896]{3,0,2,1:T(4,128)S(1)} %pad_maximum_fusion), channel_id=1, replica_groups=mesh['cell'=8,'grp'=4] {'grp'}, dimensions={2}, use_global_device_ids=true | all-gather | bytes 161280 | tf_op jit(solution)/shard_map/all_gather | solution.py:119
  62.7 0.6 gather_fusion.2
  64.2 2.4 %while.79 = (s32[]{:T(128)}, f32[3,128]{1,0:T(4,128)S(1)}, f32[3,3,1024]{2,0,1:T(4,128)S(1)}, f32[3,3,128]{2,1,0:T(4,128)S(1)}, f32[3,3,1024]{2,1,0:T(4,128)S(1)...) while((s32[]{:T(128)}, f32[3,128]{1,0:T(4,128)S(1)}, ...), condition=%wide.region_18.22_spmd, body=%wide.region_15.21_spmd.sunk | while | flops 2375092 | bytes 91217 | solution.py:208
  66.6 0.6 fusion.190
  67.6 6.3 %while.78 = (s32[]{:T(128)}, f32[4,3,128]{2,1,0:T(4,128)S(1)}, f32[4,3,1152]{2,1,0:T(4,128)S(1)}, f32[4,3,128]{2,1,0:T(4,128)S(1)}, f32[4,3,1152]{2,1,0:T(4,128)...) while((s32[]{:T(128)}, f32[4,3,128]{2,1,0:T(4,128)S(1)}, ...), condition=%wide.region_14.17_spmd, body=%wide.region_4.16_spmd.sunk | while | flops 6232500 | bytes 724117 | solution.py:204
  68.2 0.9 fusion.208
  69.8 0.9 fusion.208
  71.4 0.9 fusion.208
  73.0 0.9 fusion.208
  74.1 1.3 collective-permute-start.5
  75.4 4.5 %collective-permute-start.4 = (f32[3,1,1,640]{3,0,2,1:T(4,128)S(1)}, f32[3,1,1,640]{3,0,2,1:T(4,128)S(1)}, u32[]{:S(2)}, u32[]{:S(2)}) collective-permute-start(f32[3,1,1,640]{3,0,2,1:T(4,128)S(1)} %maximum_bitcast_fusion.2), channel_id=1, source_target_pairs={{0,4},{4,8},{8,12},{12,16},{16,20},{20,24},{24,28},{1,5},{5,9},{9,... | collective-permute-start | bytes 23048 | tf_op jit(solution)/shard_map/ppermute | solution.py:18
  79.9 0.8 maximum_dynamic-update-slice_fusion.1
  80.7 7.0 %all-reduce.4 = f32[28]{0:T(128)S(1)} all-reduce(f32[28]{0:T(128)S(1)} %maximum_dynamic-update-slice_fusion.1), channel_id=4, replica_groups=mesh['cell'=8,'grp'=4] {'grp'}, use_global_device_ids=true, to_apply=%add.4 | all-reduce | flops 28 | bytes 224
  88.1 17.1 %all-reduce.5 = f32[56]{0:T(128)S(1)} all-reduce(f32[56]{0:T(128)S(1)} %dynamic-update-slice.3), channel_id=5, replica_groups=mesh['cell'=8,'grp'=4] {'cell'}, use_global_device_ids=true, to_apply=%add.5 | all-reduce | flops 56 | bytes 448
  105.7 5.4 %all_gather.44 = f32[3,3,4,640]{3,0,2,1:T(4,128)S(1)} all-gather(f32[3,3,1,640]{3,0,2,1:T(4,128)S(1)} %pad_maximum_fusion.2), channel_id=1, replica_groups=mesh['cell'=8,'grp'=4] {'grp'}, dimensions={2}, use_global_device_ids=true | all-gather | bytes 115200 | tf_op jit(solution)/shard_map/all_gather | solution.py:119
  113.2 6.3 %while.80 = (s32[]{:T(128)}, f32[4,3,128]{2,1,0:T(4,128)S(1)}, f32[4,3,1152]{2,1,0:T(4,128)S(1)}, f32[4,3,128]{2,1,0:T(4,128)S(1)}, f32[4,3,1152]{2,1,0:T(4,128)...) while((s32[]{:T(128)}, f32[4,3,128]{2,1,0:T(4,128)S(1)}, ...), condition=%wide.region_33.37_spmd, body=%wide.region_23.36_spmd.sunk | while | flops 6232500 | bytes 724117 | solution.py:204
  113.9 0.9 fusion.213
  115.5 0.9 fusion.213
  117.1 0.9 fusion.213
  118.6 0.9 fusion.213
  119.7 2.4 %while.81 = (s32[]{:T(128)}, f32[3,128]{1,0:T(4,128)S(1)}, f32[3,3,1024]{2,0,1:T(4,128)S(1)}, f32[3,3,128]{2,1,0:T(4,128)S(1)}, f32[3,3,1024]{2,1,0:T(4,128)S(1)...) while((s32[]{:T(128)}, f32[3,128]{1,0:T(4,128)S(1)}, ...), condition=%wide.region_37.41_spmd, body=%wide.region_34.40_spmd.sunk | while | flops 2375092 | bytes 91217 | solution.py:208
  122.9 1.3 collective-permute-start.7
  124.2 4.5 %collective-permute-start.6 = (f32[3,1,1,640]{3,0,2,1:T(4,128)S(1)}, f32[3,1,1,640]{3,0,2,1:T(4,128)S(1)}, u32[]{:S(2)}, u32[]{:S(2)}) collective-permute-start(f32[3,1,1,640]{3,0,2,1:T(4,128)S(1)} %maximum_bitcast_fusion.3), channel_id=1, source_target_pairs={{0,4},{4,8},{8,12},{12,16},{16,20},{20,24},{24,28},{1,5},{5,9},{9,... | collective-permute-start | bytes 23048 | tf_op jit(solution)/shard_map/ppermute | solution.py:18
  128.8 0.8 maximum_dynamic-update-slice_fusion.2
  129.6 5.7 %all-reduce.6 = f32[28]{0:T(128)S(1)} all-reduce(f32[28]{0:T(128)S(1)} %maximum_dynamic-update-slice_fusion.2), channel_id=6, replica_groups=mesh['cell'=8,'grp'=4] {'grp'}, use_global_device_ids=true, to_apply=%add.6 | all-reduce | flops 28 | bytes 224
  135.7 20.0 %all-reduce.7 = f32[56]{0:T(128)S(1)} all-reduce(f32[56]{0:T(128)S(1)} %dynamic-update-slice.5), channel_id=7, replica_groups=mesh['cell'=8,'grp'=4] {'cell'}, use_global_device_ids=true, to_apply=%add.7 | all-reduce | flops 56 | bytes 448
  156.2 5.4 %all_gather.48 = f32[3,3,4,640]{3,0,2,1:T(4,128)S(1)} all-gather(f32[3,3,1,640]{3,0,2,1:T(4,128)S(1)} %pad_maximum_fusion.3), channel_id=1, replica_groups=mesh['cell'=8,'grp'=4] {'grp'}, dimensions={2}, use_global_device_ids=true | all-gather | bytes 115200 | tf_op jit(solution)/shard_map/all_gather | solution.py:119
  162.2 0.6 gather_fusion.9
  163.7 6.3 %while.82 = (s32[]{:T(128)}, f32[4,3,128]{2,1,0:T(4,128)S(1)}, f32[4,3,1152]{2,1,0:T(4,128)S(1)}, f32[4,3,128]{2,1,0:T(4,128)S(1)}, f32[4,3,1152]{2,1,0:T(4,128)...) while((s32[]{:T(128)}, f32[4,3,128]{2,1,0:T(4,128)S(1)}, ...), condition=%wide.region_52.56_spmd, body=%wide.region_42.55_spmd.sunk | while | flops 6232500 | bytes 724117 | solution.py:204
  164.4 0.9 fusion.218
  166.0 0.9 fusion.218
  167.6 0.9 fusion.218
  169.1 0.9 fusion.218
  170.7 2.4 %while.83 = (s32[]{:T(128)}, f32[3,128]{1,0:T(4,128)S(1)}, f32[3,3,1024]{2,0,1:T(4,128)S(1)}, f32[3,3,128]{2,1,0:T(4,128)S(1)}, f32[3,3,1024]{2,1,0:T(4,128)S(1)...) while((s32[]{:T(128)}, f32[3,128]{1,0:T(4,128)S(1)}, ...), condition=%wide.region_56.60_spmd, body=%wide.region_53.59_spmd.sunk | while | flops 2375092 | bytes 91217 | solution.py:208
  (394 shorter events, 27.9 us)
Async XLA Ops:
  0.6 7.5 %copy-start = (f32[3,384]{1,0:T(4,128)S(1)}, f32[3,384]{1,0:T(4,128)}, u32[]{:S(2)}) copy-start(f32[3,384]{1,0:T(4,128)} %param.29) | copy-start | bytes 13828
  0.6 7.5 %copy-start.1 = (f32[3,512]{1,0:T(4,128)S(1)}, f32[3,512]{1,0:T(4,128)}, u32[]{:S(2)}) copy-start(f32[3,512]{1,0:T(4,128)} %param.28) | copy-start | bytes 18436
  1.4 47.7 %collective-permute-start.1 = (f32[3,1,1,640]{3,0,2,1:T(4,128)S(1)}, f32[3,1,1,640]{3,0,2,1:T(4,128)S(1)}, u32[]{:S(2)}, u32[]{:S(2)}) collective-permute-start(f32[3,1,1,640]{3,0,2,1:T(4,128)S(1)} %maximum_bitcast_fusion.1), channel_id=1, source_target_pairs={{4,0},{8,4},{12,8},{16,12},{20,16},{24,20},{28,24},{5,1},{9,5},{13... | collective-permute-start | bytes 23048 | tf_op jit(solution)/shard_map/ppermute | solution.py:19
  2.7 46.4 %collective-permute-start = (f32[3,1,1,640]{3,0,2,1:T(4,128)S(1)}, f32[3,1,1,640]{3,0,2,1:T(4,128)S(1)}, u32[]{:S(2)}, u32[]{:S(2)}) collective-permute-start(f32[3,1,1,640]{3,0,2,1:T(4,128)S(1)} %maximum_bitcast_fusion.1), channel_id=1, source_target_pairs={{0,4},{4,8},{8,12},{12,16},{16,20},{20,24},{24,28},{1,5},{5,9},{9,... | collective-permute-start | bytes 23048 | tf_op jit(solution)/shard_map/ppermute | solution.py:18
  8.2 6.8 %copy-start.7 = (s32[4,4]{1,0:T(4,128)S(1)}, s32[4,4]{1,0:T(4,128)}, u32[]{:S(2)}) copy-start(s32[4,4]{1,0:T(4,128)} %param.36) | copy-start | bytes 196
  8.2 48.2 %collective-permute-start.3 = (f32[3,1,1,896]{3,0,2,1:T(4,128)S(1)}, f32[3,1,1,896]{3,0,2,1:T(4,128)S(1)}, u32[]{:S(2)}, u32[]{:S(2)}) collective-permute-start(f32[3,1,1,896]{3,0,2,1:T(4,128)S(1)} %maximum_bitcast_fusion), channel_id=1, source_target_pairs={{4,0},{8,4},{12,8},{16,12},{20,16},{24,20},{28,24},{5,1},{9,5},{13... | collective-permute-start | bytes 32264 | tf_op jit(solution)/shard_map/ppermute | solution.py:19
  9.5 46.9 %collective-permute-start.2 = (f32[3,1,1,896]{3,0,2,1:T(4,128)S(1)}, f32[3,1,1,896]{3,0,2,1:T(4,128)S(1)}, u32[]{:S(2)}, u32[]{:S(2)}) collective-permute-start(f32[3,1,1,896]{3,0,2,1:T(4,128)S(1)} %maximum_bitcast_fusion), channel_id=1, source_target_pairs={{0,4},{4,8},{8,12},{12,16},{16,20},{20,24},{24,28},{1,5},{5,9},{9,... | collective-permute-start | bytes 32264 | tf_op jit(solution)/shard_map/ppermute | solution.py:18
  15.0 0.7 copy-start.8
  15.7 0.7 copy-start.2
  15.8 1.3 copy-start.4
  17.0 0.7 copy-start.11
  17.7 0.7 copy-start.10
  47.5 0.7 copy-start.9
  64.2 2.4 %copy-start.5 = (f32[384]{0:T(512)S(1)}, f32[384]{0:T(512)}, u32[]{:S(2)}) copy-start(f32[384]{0:T(512)} %param.34) | copy-start | bytes 4612
  67.5 6.4 %copy-start.3 = (f32[3,512]{1,0:T(4,128)S(1)}, f32[3,512]{1,0:T(4,128)}, u32[]{:S(2)}) copy-start(f32[3,512]{1,0:T(4,128)} %param.31) | copy-start | bytes 18436
  67.5 6.4 %copy-start.6 = (f32[512]{0:T(512)S(1)}, f32[512]{0:T(512)}, u32[]{:S(2)}) copy-start(f32[512]{0:T(512)} %param.32) | copy-start | bytes 6148
  74.1 31.6 %collective-permute-start.5 = (f32[3,1,1,640]{3,0,2,1:T(4,128)S(1)}, f32[3,1,1,640]{3,0,2,1:T(4,128)S(1)}, u32[]{:S(2)}, u32[]{:S(2)}) collective-permute-start(f32[3,1,1,640]{3,0,2,1:T(4,128)S(1)} %maximum_bitcast_fusion.2), channel_id=1, source_target_pairs={{4,0},{8,4},{12,8},{16,12},{20,16},{24,20},{28,24},{5,1},{9,5},{13... | collective-permute-start | bytes 23048 | tf_op jit(solution)/shard_map/ppermute | solution.py:19
  75.4 30.3 %collective-permute-start.4 = (f32[3,1,1,640]{3,0,2,1:T(4,128)S(1)}, f32[3,1,1,640]{3,0,2,1:T(4,128)S(1)}, u32[]{:S(2)}, u32[]{:S(2)}) collective-permute-start(f32[3,1,1,640]{3,0,2,1:T(4,128)S(1)} %maximum_bitcast_fusion.2), channel_id=1, source_target_pairs={{0,4},{4,8},{8,12},{12,16},{16,20},{20,24},{24,28},{1,5},{5,9},{9,... | collective-permute-start | bytes 23048 | tf_op jit(solution)/shard_map/ppermute | solution.py:18
  122.9 33.3 %collective-permute-start.7 = (f32[3,1,1,640]{3,0,2,1:T(4,128)S(1)}, f32[3,1,1,640]{3,0,2,1:T(4,128)S(1)}, u32[]{:S(2)}, u32[]{:S(2)}) collective-permute-start(f32[3,1,1,640]{3,0,2,1:T(4,128)S(1)} %maximum_bitcast_fusion.3), channel_id=1, source_target_pairs={{4,0},{8,4},{12,8},{16,12},{20,16},{24,20},{28,24},{5,1},{9,5},{13... | collective-permute-start | bytes 23048 | tf_op jit(solution)/shard_map/ppermute | solution.py:19
  124.2 32.0 %collective-permute-start.6 = (f32[3,1,1,640]{3,0,2,1:T(4,128)S(1)}, f32[3,1,1,640]{3,0,2,1:T(4,128)S(1)}, u32[]{:S(2)}, u32[]{:S(2)}) collective-permute-start(f32[3,1,1,640]{3,0,2,1:T(4,128)S(1)} %maximum_bitcast_fusion.3), channel_id=1, source_target_pairs={{0,4},{4,8},{8,12},{12,16},{16,20},{20,24},{24,28},{1,5},{5,9},{9,... | collective-permute-start | bytes 23048 | tf_op jit(solution)/shard_map/ppermute | solution.py:18
